TPU v7x, 32 devices: a whole 2x2x4 slice. The times are simulated.
32 devices in a mesh: shard: 8 (over z, x), rep: 4 (over y, core).
Axes of the slice: x: 2, y: 2, z: 4, core: 2. Of those that a mesh axis runs over, the one named last changes fastest.
Arguments:
- lender_block: int32 [96, 8], P(('shard', 'rep')), may hold values from 0 to 255, as said below
- confidence: bfloat16 [96, 8, 256, 256], P(('shard', 'rep')), may hold values from 0 to 80, as said below
- lender_factors: bfloat16 [65536, 128], P('shard'), may hold values from -4 to 4
Outputs:
- borrower_factors: float32 [24576, 128], P(('shard', 'rep'))
- lender_rhs: float32 [65536, 128], P('shard')
Inputs may be any that keep to these rules, and one draw needn't show every extreme that they name: `lender_block`: within one device's 3 borrower blocks, at most 6 of the 3 x 8 entries name blocks of any one owner (block // 32), and on every device some owner is named exactly 6 times. `confidence`: about half the entries are zero; the others are positive.
All inputs are finite; a program needn't handle non-finite values.
Results may differ from a plain program's by a relative error of at most 0.0047.
Values may be sent and summed in bfloat16 or wider, within the bound.
A program may use at most 128 MiB of HBM per device.

v0:
```python
import jax
import jax.numpy as jnp
from jax import lax
from jax.sharding import PartitionSpec as P

CG_STEPS = 3
HIGH = lax.Precision.HIGHEST


def apply_system(direction, confidence, fetched, gram):
    low = direction.astype(jnp.bfloat16)
    scores = jnp.einsum("btr,bklr->bktl", low, fetched, preferred_element_type=jnp.float32)
    weighted = (confidence.astype(jnp.float32) * scores).astype(jnp.bfloat16)
    back = jnp.einsum("bktl,bklr->btr", weighted, fetched, preferred_element_type=jnp.float32)
    width = direction.shape[-1]
    global_part = jnp.dot(
        direction.reshape(-1, width), gram, precision=HIGH, preferred_element_type=jnp.float32
    )
    return global_part.reshape(direction.shape) + 0.1 * direction + back


def per_device(lender_block, confidence, lender_factors):
    shards = lax.axis_size("shard")
    blocks, lists = lender_block.shape
    tile = confidence.shape[2]
    rank = lender_factors.shape[1]
    owned = lender_factors.shape[0] // tile
    entries = blocks * lists
    slots = (2 * entries + shards - 1) // shards
    local_gram = lax.dot_general(
        lender_factors, lender_factors, (((0,), (0,)), ((), ())), preferred_element_type=jnp.float32
    )
    gram = lax.psum(local_gram, "shard")
    flat = lender_block.reshape(entries)
    owner = flat // owned
    within = flat - owner * owned
    member = (owner[:, None] == jnp.arange(shards, dtype=jnp.int32)[None, :]).astype(jnp.int32)
    position = jnp.sum(jnp.cumsum(member, axis=0) * member, axis=1) - 1
    slot_index = owner * slots + position
    requests = (
        jnp.zeros((shards * slots,), jnp.int32).at[slot_index].set(within).reshape(shards, slots)
    )
    table = lender_factors.reshape(owned, tile, rank)
    incoming = lax.all_to_all(requests, "shard", split_axis=0, concat_axis=0, tiled=True)
    replies = lax.all_to_all(table[incoming], "shard", split_axis=0, concat_axis=0, tiled=True)
    fetched = replies.reshape(shards * slots, tile, rank)[slot_index].reshape(
        blocks, lists, tile, rank
    )
    rhs = jnp.einsum("bktl,bklr->btr", confidence, fetched, preferred_element_type=jnp.float32)
    solution = jnp.zeros_like(rhs)
    resid = rhs
    direction = rhs
    norm_now = jnp.sum(resid * resid, axis=2, keepdims=True)
    for count in range(CG_STEPS):
        image = apply_system(direction, confidence, fetched, gram)
        alpha = norm_now / (jnp.sum(direction * image, axis=2, keepdims=True) + 1e-06)
        solution = solution + alpha * direction
        resid = resid - alpha * image
        norm_next = jnp.sum(resid * resid, axis=2, keepdims=True)
        direction = resid + norm_next / (norm_now + 1e-06) * direction
        norm_now = norm_next
    solved = solution.astype(jnp.bfloat16)
    partial_rhs = jnp.einsum(
        "bktl,btr->bklr", confidence, solved, preferred_element_type=jnp.float32
    )
    outgoing = (
        jnp.zeros((shards * slots, tile, rank), jnp.float32)
        .at[slot_index]
        .set(partial_rhs.reshape(entries, tile, rank))
    )
    returned = lax.all_to_all(
        outgoing.reshape(shards, slots, tile, rank),
        "shard",
        split_axis=0,
        concat_axis=0,
        tiled=True,
    )
    selector = (
        incoming.reshape(-1)[None, :] == jnp.arange(owned, dtype=jnp.int32)[:, None]
    ).astype(jnp.float32)
    owner_sum = jnp.dot(
        selector,
        returned.reshape(shards * slots, tile * rank),
        precision=HIGH,
        preferred_element_type=jnp.float32,
    )
    total = lax.psum(owner_sum, "rep")
    lenders_all = owned * tile * shards
    lender_rhs = total.reshape(owned * tile, rank) / lenders_all
    return (solution.reshape(blocks * tile, rank), lender_rhs)


def solution(mesh):
    in_specs = (P(("shard", "rep"), None), P(("shard", "rep"), None, None, None), P("shard", None))
    out_specs = (P(("shard", "rep"), None), P("shard", None))
    return jax.shard_map(
        per_device, mesh=mesh, in_specs=in_specs, out_specs=out_specs, check_vma=False
    )
```

profile of v0, /device:TPU:0, one launch (start us, length us, event | category | flops | bytes accessed | tf_op | source)
XLA Modules:
  0.0 416.2 jit_solution(9014133852448018927)
XLA Ops:
  7.2 0.9 reshape.224
  8.1 0.8 reshape.223
  9.2 0.6 scatter_custom_fusion
  9.9 13.6 %all_to_all.22 = s32[8,1,6]{2,1,0:T(1,128)S(1)} all-to-all(s32[8,1,6]{2,1,0:T(1,128)S(1)} %bitcast.112), channel_id=1, replica_groups=mesh['shard'=8,'rep'=4] {'shard'}, dimensions={0} | all-to-all | bytes 384 | tf_op jit(solution)/shard_map/all_to_all | solution.py:44
  23.8 2.7 gather_fusion
  26.5 4.4 %all-to-all-start.1 = ((bf16[8,6,256,128]{3,2,1,0:T(8,128)(2,1)}), bf16[8,6,256,128]{3,2,1,0:T(8,128)(2,1)}, u32[]{:S(2)}, u32[]{:S(2)}) async-start(bf16[8,6,256,128]{3,2,1,0:T(8,128)(2,1)} %bitcast.106), calls=%async_computation.1 | async-start | bytes 6291456 | tf_op jit(solution)/shard_map/all_to_all | solution.py:45
  31.0 1.4 fusion.55
  32.4 4.7 %copy.37 = bf16[3,8,256,256]{2,3,1,0:T(8,128)(2,1)} copy(bf16[3,8,256,256]{3,2,1,0:T(8,128)(2,1)} %param.4) | data formatting | bytes 6291456 | tf_op args[1]
  37.1 64.9 %all-to-all-done.1 = bf16[8,6,256,128]{3,2,1,0:T(8,128)(2,1)} async-done(((bf16[8,6,256,128]{3,2,1,0:T(8,128)(2,1)}), bf16[8,6,256,128]{3,2,1,0:T(8,128)(2,1)}, u32[]{:S(2)}, u32[]{:S(2)}) %all-to-all-start.1) | async-done | bytes 3145760 | tf_op jit(solution)/shard_map/all_to_all | solution.py:45
  102.0 3.8 gather_fusion.1
  105.8 3.5 convolution_bitcast_fusion
  109.4 4.3 %fusion.18 = f32[3,256,128]{1,2,0:T(8,128)S(1)} fusion(bf16[3,8,256,128]{3,2,1,0:T(8,128)(2,1)} %bitcast.108, bf16[3,8,256,256]{2,3,1,0:T(8,128)(2,1)} %copy.37, f32[3,256,128]{1,2,0:T(8,128)S(1)} %convolution_bitcast_fusion), kind=kOutput, calls=%fused_computation.20 | convolution fusion | flops 810123264 | bytes 5505024 | tf_op jit(solution)/shard_map/bktl,bklr->btr/dot_general | solution.py:14
  113.7 13.5 %all-reduce.3.cloned.1.call-done = f32[128,128]{1,0:T(8,128)} async-done(((f32[128,128]{1,0:T(8,128)}), f32[128,128]{1,0:T(8,128)}) %all-reduce.3.cloned.1.call-update) | async-done | bytes 65552 | tf_op jit(solution)/shard_map/psum | solution.py:33
  127.2 1.4 multiply_reduce_fusion.3
  128.8 5.1 %fusion.21 = f32[3,256,128]{1,2,0:T(8,128)} fusion(bf16[3,8,256,128]{3,2,1,0:T(8,128)(2,1)} %bitcast.109, bf16[3,8,256,256]{2,3,1,0:T(8,128)(2,1)} %copy.37, f32[3,256,128]{1,2,0:T(8,128)S(1)} %multiply_add_fusion.2), kind=kOutput, calls=%fused_computation.21 | convolution fusion | flops 810123264 | bytes 5505024 | tf_op jit(solution)/shard_map/bktl,bklr->btr/dot_general | solution.py:14
  133.8 1.6 multiply_reduce_fusion.1
  135.5 0.8 multiply_add_fusion.1
  136.3 5.2 %fusion.24 = f32[3,256,128]{1,2,0:T(8,128)} fusion(bf16[3,8,256,128]{3,2,1,0:T(8,128)(2,1)} %bitcast.110, bf16[3,8,256,256]{2,3,1,0:T(8,128)(2,1)} %copy.37, f32[3,256,128]{1,2,0:T(8,128)} %multiply_add_fusion.1), kind=kOutput, calls=%fused_computation.22 | convolution fusion | flops 810123264 | bytes 5505024 | tf_op jit(solution)/shard_map/bktl,bklr->btr/dot_general | solution.py:14
  141.5 1.6 fusion.31
  143.1 1.1 multiply_add_fusion
  144.2 4.1 fusion.38
  148.3 3.6 copy.52
  151.9 3.4 broadcast_in_dim.5
  155.3 7.9 %scatter_fusion = f32[48,256,128]{2,1,0:T(8,128)} fusion(f32[48,256,128]{2,1,0:T(8,128)} %broadcast_in_dim.5, s32[24]{0:T(128)S(1)} %fusion.52, f32[24,256,128]{2,1,0:T(8,128)} %copy.52), kind=kCustom, calls=%fused_computation.3 | custom fusion | bytes 9437280 | tf_op jit(solution)/shard_map/scatter | solution.py:69
  163.3 4.8 %all-to-all-start.2 = ((f32[8,6,256,128]{3,2,1,0:T(8,128)}), f32[8,6,256,128]{3,2,1,0:T(8,128)}, u32[]{:S(2)}, u32[]{:S(2)}) async-start(f32[8,6,256,128]{3,2,1,0:T(8,128)} %bitcast.104), calls=%async_computation.2 | async-start | bytes 12582912 | tf_op jit(solution)/shard_map/all_to_all | solution.py:71
  168.8 0.7 reduce.3
  169.5 135.1 %all-to-all-done.2 = f32[8,6,256,128]{3,2,1,0:T(8,128)} async-done(((f32[8,6,256,128]{3,2,1,0:T(8,128)}), f32[8,6,256,128]{3,2,1,0:T(8,128)}, u32[]{:S(2)}, u32[]{:S(2)}) %all-to-all-start.2) | async-done | bytes 6291488 | tf_op jit(solution)/shard_map/all_to_all | solution.py:71
  304.6 10.8 %fusion.3 = f32[32,32768]{1,0:T(8,128)} fusion(f32[6,8,256,128]{3,2,1,0:T(8,128)} %bitcast.40, s32[48]{0:T(128)S(1)} %eq.31), kind=kOutput, calls=%fused_computation.10 | convolution fusion | flops 603981312 | bytes 10485952 | tf_op jit(solution)/shard_map/dot_general | solution.py:81
  315.4 0.9 copy.51
  316.3 83.7 %all-reduce.5.cloned.1.call-done = f32[32,32768]{1,0:T(8,128)} async-done(((f32[32,32768]{1,0:T(8,128)}), f32[32,32768]{1,0:T(8,128)}) %all-reduce.5.cloned.1.call-update) | async-done | bytes 4194320 | tf_op jit(solution)/shard_map/psum | solution.py:87
  400.0 4.4 %broadcast_multiply_fusion = f32[32,32768]{1,0:T(8,128)} fusion(f32[32,32768]{1,0:T(8,128)} %all-reduce.5.cloned.1.call-done), kind=kLoop, calls=%fused_computation.19 | loop fusion | flops 1048576 | bytes 8388608 | tf_op jit(solution)/shard_map/div | solution.py:89
  404.5 4.9 %div.83 = f32[8192,128]{1,0:T(8,128)} reshape(f32[32,32768]{1,0:T(8,128)} %broadcast_multiply_fusion) | data formatting | bytes 8388608 | tf_op jit(solution)/shard_map/div | solution.py:89
  (32 shorter events, 1.8 us)
Async XLA Ops:
  7.2 16.6 %copy-start = (bf16[8192,128]{1,0:T(8,128)(2,1)S(1)}, bf16[8192,128]{1,0:T(8,128)(2,1)}, u32[]{:S(2)}) copy-start(bf16[8192,128]{1,0:T(8,128)(2,1)} %param.5) | copy-start | bytes 6291460
  26.5 75.5 %all-to-all-start.1 = ((bf16[8,6,256,128]{3,2,1,0:T(8,128)(2,1)}), bf16[8,6,256,128]{3,2,1,0:T(8,128)(2,1)}, u32[]{:S(2)}, u32[]{:S(2)}) async-start(bf16[8,6,256,128]{3,2,1,0:T(8,128)(2,1)} %bitcast.106), calls=%async_computation.1 | async-start | bytes 6291456 | tf_op jit(solution)/shard_map/all_to_all | solution.py:45
  30.9 96.2 %all-reduce.3.cloned.1.call-start = ((), (), s32[]{:S(2)}) async-start(), calls=%async_computation.3 | async-start | bytes 131072 | tf_op jit(solution)/shard_map/psum | solution.py:33
  128.7 5.1 %copy-start.2 = (f32[128,128]{1,0:T(8,128)S(1)}, f32[128,128]{1,0:T(8,128)}, u32[]{:S(2)}) copy-start(f32[128,128]{1,0:T(8,128)} %all-reduce.3.cloned.1.call-done) | copy-start | bytes 196612
  136.3 5.2 %copy-start.1 = (f32[3,256,128]{1,2,0:T(8,128)S(1)}, f32[3,256,128]{1,2,0:T(8,128)}, u32[]{:S(2)}) copy-start(f32[3,256,128]{1,2,0:T(8,128)} %multiply_add_fusion.1) | copy-start | bytes 1179652
  163.3 141.3 %all-to-all-start.2 = ((f32[8,6,256,128]{3,2,1,0:T(8,128)}), f32[8,6,256,128]{3,2,1,0:T(8,128)}, u32[]{:S(2)}, u32[]{:S(2)}) async-start(f32[8,6,256,128]{3,2,1,0:T(8,128)} %bitcast.104), calls=%async_computation.2 | async-start | bytes 12582912 | tf_op jit(solution)/shard_map/all_to_all | solution.py:71
  168.0 232.0 %all-reduce.5.cloned.1.call-start = ((), (), s32[]{:S(2)}) async-start(), calls=%async_computation.4 | async-start | bytes 8388608 | tf_op jit(solution)/shard_map/psum | solution.py:87
Sparse Core Ops, SparseCore 0:
  35.7 91.3 all-reduce.2
  315.5 84.4 all-reduce.4
where the time goes:
time: 417 us; the launch traced here: 416 us
  waiting for transfers between devices  297 us (71%)
  matrix products  39 us (9%)
  local copies, waits for them, and re-layouts  35.2 us (8%)
  between operations  14.2 us (3%)
  blocking collectives  13.6 us (3%)
  starting transfers between devices  9.46 us (2%)
  other arithmetic  7.59 us (2%)
    all_to_all x1, waiting for transfers between devices, per_device(): lax.all_to_all(outgoing.reshape(shards, slots, tile, rank), 'shard', spli...  135 us
    psum x1, waiting for transfers between devices, per_device(): total = lax.psum(owner_sum, 'rep')  83.7 us
    all_to_all x1, waiting for transfers between devices, per_device(): lax.all_to_all(table[incoming], 'shard', split_axis=0, concat_axis=0, til...  64.9 us
    dot_general x3, matrix products, apply_system(): jnp.einsum('bktl,bklr->btr', weighted, fetched, preferred_element_type=jn...  14.5 us
    all_to_all x1, blocking collectives, per_device(): lax.all_to_all(requests, 'shard', split_axis=0, concat_axis=0, tiled=True)  13.6 us
    psum x1, waiting for transfers between devices, per_device(): gram = lax.psum(local_gram, 'shard')  13.5 us
    dot_general x1, matrix products, per_device(): jnp.dot(selector, returned.reshape(shards * slots, tile * rank), precisio...  10.8 us
  transfers between devices with their start and end apart: 4, of which 4 were waited for; matrix products, arithmetic and copies ran while one was open for 5% of the time, Pallas kernels for 0%

commit v1 on v0

--- a/solution.py
+++ b/solution.py
@@ -30,7 +30,7 @@
     local_gram = lax.dot_general(
         lender_factors, lender_factors, (((0,), (0,)), ((), ())), preferred_element_type=jnp.float32
     )
-    gram = lax.psum(local_gram, "shard")
+    gram = jnp.sum(lax.all_gather(local_gram, "shard"), axis=0)
     flat = lender_block.reshape(entries)
     owner = flat // owned
     within = flat - owner * owned

time: 417 us -> 419 us (level)
  blocking collectives: 13.6 us -> 98.7 us
  waiting for transfers between devices: 297 us -> 216 us
    all_gather x0 -> x1, blocking collectives: none -> 85.2 us  [per_device(): gram = jnp.sum(lax.all_gather(local_gram, 'shard'), axis=0)]
    all_to_all x1, waiting for transfers between devices: 64.9 us -> 0.01 us  [per_device(): lax.all_to_all(table[incoming], 'shard', split_axis=0, concat_axis=0, til...]
    psum x1 -> x0, waiting for transfers between devices: 13.5 us -> none  [per_device(): gram = lax.psum(local_gram, 'shard')]
  transfers between devices with their start and end apart: 4 -> 3, of which waited for: 4 -> 2; matrix products, arithmetic and copies ran while one was open for 5% -> 2% of each run, Pallas kernels for 0% -> 0%
where the time goes in v1:
time: 419 us; the launch traced here: 418 us
  waiting for transfers between devices  216 us (52%)
  blocking collectives  98.7 us (24%)
  matrix products  37.5 us (9%)
  local copies, waits for them, and re-layouts  35.2 us (8%)
  between operations  14.2 us (3%)
  starting transfers between devices  9.42 us (2%)
  other arithmetic  7.62 us (2%)
    all_to_all x1, waiting for transfers between devices, per_device(): lax.all_to_all(outgoing.reshape(shards, slots, tile, rank), 'shard', spli...  132 us
    all_gather x1, blocking collectives, per_device(): gram = jnp.sum(lax.all_gather(local_gram, 'shard'), axis=0)  85.2 us
    psum x1, waiting for transfers between devices, per_device(): total = lax.psum(owner_sum, 'rep')  83.7 us
    dot_general x3, matrix products, apply_system(): jnp.einsum('bktl,bklr->btr', weighted, fetched, preferred_element_type=jn...  14.5 us
    all_to_all x1, blocking collectives, per_device(): lax.all_to_all(requests, 'shard', split_axis=0, concat_axis=0, tiled=True)  13.6 us
    dot_general x1, matrix products, per_device(): jnp.dot(selector, returned.reshape(shards * slots, tile * rank), precisio...  10.8 us
  transfers between devices with their start and end apart: 3, of which 2 were waited for; matrix products, arithmetic and copies ran while one was open for 2% of the time, Pallas kernels for 0%

profile of v1, /device:TPU:0, one launch (start us, length us, event | category | flops | bytes accessed | tf_op | source)
XLA Modules:
  0.0 418.2 jit_solution(11923799878584432541)
XLA Ops:
  7.2 0.9 reshape.224
  8.1 0.8 reshape.223
  9.2 0.6 scatter_custom_fusion
  9.9 13.6 %all_to_all.22 = s32[8,1,6]{2,1,0:T(1,128)S(1)} all-to-all(s32[8,1,6]{2,1,0:T(1,128)S(1)} %bitcast.114), channel_id=1, replica_groups=mesh['shard'=8,'rep'=4] {'shard'}, dimensions={0} | all-to-all | bytes 384 | tf_op jit(solution)/shard_map/all_to_all | solution.py:44
  23.8 2.7 gather_fusion
  26.5 4.4 %all-to-all-start.1 = ((bf16[8,6,256,128]{3,2,1,0:T(8,128)(2,1)}), bf16[8,6,256,128]{3,2,1,0:T(8,128)(2,1)}, u32[]{:S(2)}, u32[]{:S(2)}) async-start(bf16[8,6,256,128]{3,2,1,0:T(8,128)(2,1)} %bitcast.107), calls=%async_computation.1 | async-start | bytes 6291456 | tf_op jit(solution)/shard_map/all_to_all | solution.py:45
  30.9 4.7 %copy.39 = bf16[3,8,256,256]{2,3,1,0:T(8,128)(2,1)} copy(bf16[3,8,256,256]{3,2,1,0:T(8,128)(2,1)} %param.4) | data formatting | bytes 6291456 | tf_op args[1]
  35.6 0.7 fusion.55
  36.4 85.2 %all-gather = f32[1024,128]{1,0:T(8,128)S(1)} all-gather(f32[128,128]{1,0:T(8,128)S(1)} %fusion.55), channel_id=2, replica_groups=mesh['shard'=8,'rep'=4] {'shard'}, dimensions={0}, use_global_device_ids=true | all-gather | bytes 589824 | tf_op jit(solution)/shard_map/all_gather | solution.py:33
  121.6 3.8 gather_fusion.1
  125.4 3.5 convolution_bitcast_fusion
  129.0 4.3 %fusion.18 = f32[3,256,128]{1,2,0:T(8,128)S(1)} fusion(bf16[3,8,256,128]{3,2,1,0:T(8,128)(2,1)} %bitcast.109, bf16[3,8,256,256]{2,3,1,0:T(8,128)(2,1)} %copy.39, f32[3,256,128]{1,2,0:T(8,128)S(1)} %convolution_bitcast_fusion), kind=kOutput, calls=%fused_computation.20 | convolution fusion | flops 810123264 | bytes 5505024 | tf_op jit(solution)/shard_map/bktl,bklr->btr/dot_general | solution.py:14
  133.3 0.6 multiply_reduce_fusion.3
  134.0 5.0 %fusion.21 = f32[3,256,128]{1,2,0:T(8,128)} fusion(bf16[3,8,256,128]{3,2,1,0:T(8,128)(2,1)} %bitcast.110, bf16[3,8,256,256]{2,3,1,0:T(8,128)(2,1)} %copy.39, f32[3,256,128]{1,2,0:T(8,128)S(1)} %multiply_add_fusion.2), kind=kOutput, calls=%fused_computation.21 | convolution fusion | flops 810123264 | bytes 5505024 | tf_op jit(solution)/shard_map/bktl,bklr->btr/dot_general | solution.py:14
  139.1 1.6 multiply_reduce_fusion.1
  140.7 0.8 multiply_add_fusion.1
  141.6 5.2 %fusion.24 = f32[3,256,128]{1,2,0:T(8,128)} fusion(bf16[3,8,256,128]{3,2,1,0:T(8,128)(2,1)} %bitcast.111, bf16[3,8,256,256]{2,3,1,0:T(8,128)(2,1)} %copy.39, f32[3,256,128]{1,2,0:T(8,128)} %multiply_add_fusion.1), kind=kOutput, calls=%fused_computation.22 | convolution fusion | flops 810123264 | bytes 5505024 | tf_op jit(solution)/shard_map/bktl,bklr->btr/dot_general | solution.py:14
  146.8 1.6 fusion.31
  148.3 1.1 multiply_add_fusion
  149.4 4.1 fusion.38
  153.6 3.6 copy.54
  157.2 3.4 broadcast_in_dim.5
  160.6 7.9 %scatter_fusion = f32[48,256,128]{2,1,0:T(8,128)} fusion(f32[48,256,128]{2,1,0:T(8,128)} %broadcast_in_dim.5, s32[24]{0:T(128)S(1)} %fusion.52, f32[24,256,128]{2,1,0:T(8,128)} %copy.54), kind=kCustom, calls=%fused_computation.3 | custom fusion | bytes 9437280 | tf_op jit(solution)/shard_map/scatter | solution.py:69
  168.5 4.8 %all-to-all-start.2 = ((f32[8,6,256,128]{3,2,1,0:T(8,128)}), f32[8,6,256,128]{3,2,1,0:T(8,128)}, u32[]{:S(2)}, u32[]{:S(2)}) async-start(f32[8,6,256,128]{3,2,1,0:T(8,128)} %bitcast.105), calls=%async_computation.2 | async-start | bytes 12582912 | tf_op jit(solution)/shard_map/all_to_all | solution.py:71
  173.5 0.5 broadcast.206
  174.0 0.7 reduce.3
  174.7 131.8 %all-to-all-done.2 = f32[8,6,256,128]{3,2,1,0:T(8,128)} async-done(((f32[8,6,256,128]{3,2,1,0:T(8,128)}), f32[8,6,256,128]{3,2,1,0:T(8,128)}, u32[]{:S(2)}, u32[]{:S(2)}) %all-to-all-start.2) | async-done | bytes 6291488 | tf_op jit(solution)/shard_map/all_to_all | solution.py:71
  306.5 10.8 %fusion.3 = f32[32,32768]{1,0:T(8,128)} fusion(f32[6,8,256,128]{3,2,1,0:T(8,128)} %bitcast.41, s32[48]{0:T(128)S(1)} %eq.31), kind=kOutput, calls=%fused_computation.10 | convolution fusion | flops 603981312 | bytes 10485952 | tf_op jit(solution)/shard_map/dot_general | solution.py:81
  317.4 0.9 copy.53
  318.3 83.7 %all-reduce.2.cloned.1.call-done = f32[32,32768]{1,0:T(8,128)} async-done(((f32[32,32768]{1,0:T(8,128)}), f32[32,32768]{1,0:T(8,128)}) %all-reduce.2.cloned.1.call-update) | async-done | bytes 4194320 | tf_op jit(solution)/shard_map/psum | solution.py:87
  402.0 4.4 %broadcast_multiply_fusion = f32[32,32768]{1,0:T(8,128)} fusion(f32[32,32768]{1,0:T(8,128)} %all-reduce.2.cloned.1.call-done), kind=kLoop, calls=%fused_computation.19 | loop fusion | flops 1048576 | bytes 8388608 | tf_op jit(solution)/shard_map/div | solution.py:89
  406.5 4.9 %div.83 = f32[8192,128]{1,0:T(8,128)} reshape(f32[32,32768]{1,0:T(8,128)} %broadcast_multiply_fusion) | data formatting | bytes 8388608 | tf_op jit(solution)/shard_map/div | solution.py:89
  (29 shorter events, 1.3 us)
Async XLA Ops:
  7.2 16.6 %copy-start = (bf16[8192,128]{1,0:T(8,128)(2,1)S(1)}, bf16[8192,128]{1,0:T(8,128)(2,1)}, u32[]{:S(2)}) copy-start(bf16[8192,128]{1,0:T(8,128)(2,1)} %param.5) | copy-start | bytes 6291460
  26.5 95.1 %all-to-all-start.1 = ((bf16[8,6,256,128]{3,2,1,0:T(8,128)(2,1)}), bf16[8,6,256,128]{3,2,1,0:T(8,128)(2,1)}, u32[]{:S(2)}, u32[]{:S(2)}) async-start(bf16[8,6,256,128]{3,2,1,0:T(8,128)(2,1)} %bitcast.107), calls=%async_computation.1 | async-start | bytes 6291456 | tf_op jit(solution)/shard_map/all_to_all | solution.py:45
  141.6 5.2 %copy-start.1 = (f32[3,256,128]{1,2,0:T(8,128)S(1)}, f32[3,256,128]{1,2,0:T(8,128)}, u32[]{:S(2)}) copy-start(f32[3,256,128]{1,2,0:T(8,128)} %multiply_add_fusion.1) | copy-start | bytes 1179652
  168.5 138.0 %all-to-all-start.2 = ((f32[8,6,256,128]{3,2,1,0:T(8,128)}), f32[8,6,256,128]{3,2,1,0:T(8,128)}, u32[]{:S(2)}, u32[]{:S(2)}) async-start(f32[8,6,256,128]{3,2,1,0:T(8,128)} %bitcast.105), calls=%async_computation.2 | async-start | bytes 12582912 | tf_op jit(solution)/shard_map/all_to_all | solution.py:71
  173.3 228.8 %all-reduce.2.cloned.1.call-start = ((), (), s32[]{:S(2)}) async-start(), calls=%async_computation.3 | async-start | bytes 8388608 | tf_op jit(solution)/shard_map/psum | solution.py:87
Sparse Core Ops, SparseCore 0:
  317.5 84.4 all-reduce.1
